TPU v7x, 128 devices: a whole 4x4x4 slice. The times are simulated.
128 devices in a mesh: dp: 1, tp: 16 (over z, y), sp: 8 (over x, core).
Axes of the slice: x: 4, y: 4, z: 4, core: 2. Of those that a mesh axis runs over, the one named last changes fastest.
Arguments:
- x_tokens: bfloat16 [8192, 4096], P(('dp', 'sp'), 'tp')
- doc_ids: int32 [8192], P(('dp', 'sp'))
- w_qkv: bfloat16 [4096, 12288], P('sp', 'tp')
- w_out: bfloat16 [4096, 4096], P('sp', 'tp')
Outputs:
- output: bfloat16 [8192, 4096], P(('dp', 'sp', 'tp'))
All inputs are finite; a program needn't handle non-finite values.
Results may differ from a plain program's by a relative error of at most 0.00246272.
Values are sent between devices in bfloat16 or wider.
A program may use at most 1 GiB of HBM per device.

v0:
```python
import functools

import jax
import jax.numpy as jnp
from jax import lax
from jax.experimental import pallas as pl
from jax.experimental.pallas import tpu as pltpu
from jax.sharding import PartitionSpec as P

HEAD_DIM = 128
EXP2_SCALE = HEAD_DIM ** -0.5 * 1.4426950408889634
FLOOR = -3.0e38


def attention_kernel(qb, kb, sub, q_ref, kv_ref, segq_ref, segk_ref, segall_ref, o_ref, acc_ref, m_ref, l_ref):
    segq_row = segq_ref[0]
    lo = jnp.min(segq_row)
    hi = jnp.max(segq_row)
    seg_all = segall_ref[...]
    first = jnp.sum(jnp.where(seg_all < lo, 1.0, 0.0)).astype(jnp.int32)
    last = jnp.sum(jnp.where(seg_all <= hi, 1.0, 0.0)).astype(jnp.int32)
    one_doc = lo == hi

    acc_ref[...] = jnp.zeros_like(acc_ref)
    l_ref[...] = jnp.zeros_like(l_ref)
    m_ref[...] = jnp.full_like(m_ref, FLOOR)

    def block(j, masked):
        start = pl.multiple_of(j * kb, kb)
        k = kv_ref[pl.ds(start, kb), :HEAD_DIM]
        v = kv_ref[pl.ds(start, kb), HEAD_DIM:]
        if masked:
            segk_row = segk_ref[j]
        for i in range(qb // sub):
            rows = slice(i * sub, (i + 1) * sub)
            s = lax.dot_general(q_ref[rows, :], k, (((1,), (1,)), ((), ())), preferred_element_type=jnp.float32)
            t = s * EXP2_SCALE
            if masked:
                segq_col = jnp.broadcast_to(segq_row[:, rows], (HEAD_DIM, sub)).T
                t = jnp.where(segq_col[:, :1] == segk_row, t, -jnp.inf)
            m_prev = m_ref[rows, :1]
            m_new = jnp.maximum(m_prev, jnp.max(t, axis=1, keepdims=True))
            p = jnp.exp2(t - m_new)
            alpha = jnp.exp2(m_prev - m_new)
            l_new = l_ref[rows, :1] * alpha + jnp.sum(p, axis=1, keepdims=True)
            pv = jnp.dot(p.astype(jnp.bfloat16), v, preferred_element_type=jnp.float32)
            acc_ref[rows, :] = acc_ref[rows, :] * alpha + pv
            m_ref[rows, :] = jnp.broadcast_to(m_new, (sub, HEAD_DIM))
            l_ref[rows, :] = jnp.broadcast_to(l_new, (sub, HEAD_DIM))

    def step(j, carry):
        whole = one_doc & (j * kb >= first) & ((j + 1) * kb <= last)

        @pl.when(whole)
        def _():
            block(j, False)

        @pl.when(jnp.logical_not(whole))
        def _():
            block(j, True)

        return carry

    lax.fori_loop(first // kb, (last + kb - 1) // kb, step, 0)
    o_ref[...] = (acc_ref[...] / l_ref[...]).astype(o_ref.dtype)


def attention(q, kv, seg_q, seg_all, qb=512, kb=512, sub=256):
    rows, keys = q.shape[0], kv.shape[0]
    heads = q.shape[1] // HEAD_DIM
    return pl.pallas_call(
        functools.partial(attention_kernel, qb, kb, sub),
        grid=(heads, rows // qb),
        out_shape=jax.ShapeDtypeStruct(q.shape, jnp.bfloat16),
        in_specs=[
            pl.BlockSpec((qb, HEAD_DIM), lambda h, i: (i, h)),
            pl.BlockSpec((keys, 2 * HEAD_DIM), lambda h, i: (0, h)),
            pl.BlockSpec((1, 1, qb), lambda h, i: (i, 0, 0)),
            pl.BlockSpec((keys // kb, 1, kb), lambda h, i: (0, 0, 0)),
            pl.BlockSpec((keys // HEAD_DIM, HEAD_DIM), lambda h, i: (0, 0)),
        ],
        out_specs=pl.BlockSpec((qb, HEAD_DIM), lambda h, i: (i, h)),
        scratch_shapes=[
            pltpu.VMEM((qb, HEAD_DIM), jnp.float32),
            pltpu.VMEM((qb, HEAD_DIM), jnp.float32),
            pltpu.VMEM((qb, HEAD_DIM), jnp.float32),
        ],
        compiler_params=pltpu.CompilerParams(vmem_limit_bytes=48 * 1024 * 1024),
        name="attention",
    )(q, kv, seg_q.reshape(rows // qb, 1, qb), seg_all.reshape(keys // kb, 1, kb), seg_all.reshape(keys // HEAD_DIM, HEAD_DIM))


SIDE = 4
CHUNKS = 4
MESH = pl.DeviceIdType.MESH


def remote(src, dst, send_sem, recv_sem, tp, sp):
    return pltpu.make_async_remote_copy(
        src_ref=src, dst_ref=dst, send_sem=send_sem, recv_sem=recv_sem,
        device_id={"tp": tp, "sp": sp}, device_id_type=MESH)


def arrived(ref, sem, tp, sp):
    remote(ref, ref, sem, sem, tp, sp).wait_recv()


def barrier_with(peers):
    barrier = pltpu.get_barrier_semaphore()
    for tp, sp in peers:
        pl.semaphore_signal(barrier, inc=1, device_id={"tp": tp, "sp": sp}, device_id_type=MESH)
    pl.semaphore_wait(barrier, len(peers))


class Gather2D:
    def __init__(self, coords, place, own, held, send_sem, recv_sem):
        self.coords, self.place, self.own, self.held = coords, place, own, held
        self.send_sem, self.recv_sem = send_sem, recv_sem
        self.sent = {}

    def at(self, h, j1, j2):
        u, v = self.coords
        j1, j2 = (j1, j2) if h == 0 else (j2, j1)
        return lax.rem(u + j1, SIDE), lax.rem(v + j2, SIDE)

    def send(self, r, h, piece, to):
        src_at, dst_at = self.at(h, *piece), self.at(h, *to)
        src = self.own(r, h) if piece == (0, 0) else self.held(r, h, *src_at)
        k = self.sent.get((r, h), 0)
        self.sent[r, h] = k + 1
        copy = remote(src, self.held(r, h, *src_at), self.send_sem.at[r, h, k],
                      self.recv_sem.at[r, h, src_at[0] * SIDE + src_at[1]], *self.place(*dst_at))
        copy.start()

    def wait(self, r, h, piece):
        src_at = self.at(h, *piece)
        arrived(self.held(r, h, *src_at), self.recv_sem.at[r, h, src_at[0] * SIDE + src_at[1]], *self.place(*self.coords))

    def start(self, r):
        for h in (0, 1):
            for to in ((1, 0), (3, 0), (0, 1), (0, 3)):
                self.send(r, h, (0, 0), to)

    def spread(self, r, h, j1):
        for j2 in (1, 3):
            self.send(r, h, (j1, 0), (0, j2))

    def near(self, r):
        for j1 in (3, 1):
            for h in (0, 1):
                self.wait(r, h, (j1, 0))
                if j1 == (3 if (r + h) % 2 == 0 else 1):
                    self.send(r, h, (j1, 0), (4 - j1, 0))
                self.spread(r, h, j1)

    def pass_on(self, r, j1):
        for h in (0, 1):
            for j2 in (3, 1):
                self.wait(r, h, (j1, j2))
                if j2 == (3 if (r + h + (j1 + 1) // 2) % 2 == 0 else 1):
                    self.send(r, h, (j1, j2), (0, 4 - j2))

    def far(self, r):
        self.pass_on(r, 0)
        for h in (0, 1):
            self.wait(r, h, (2, 0))
            self.spread(r, h, 2)

    def last(self, r):
        for j1 in (3, 1, 2):
            self.pass_on(r, j1)
        for j1 in (0, 3, 1, 2):
            for h in (0, 1):
                self.wait(r, h, (j1, 2))

    def drain(self, r):
        for h in (0, 1):
            for k in range(self.sent[r, h]):
                ref = self.own(r, h)
                remote(ref, ref, self.send_sem.at[r, h, k], self.recv_sem.at[r, h, 0], *self.place(*self.coords)).wait_send()


def qkv_kernel(x_ref, w_ref, seg_ref, q_ref, kv_ref, segall_ref,
               x_all, w_all, qkv, xs, xr, ws, wr, ss, sr, ks, kr):
    tp, sp = lax.axis_index("tp"), lax.axis_index("sp")
    z, y = tp // SIDE, lax.rem(tp, SIDE)
    x, core = sp // 2, lax.rem(sp, 2)
    rows, width = x_ref.shape
    depth = w_ref.shape[0]
    chunk = rows // CHUNKS
    half = width // 2

    def sp_at(dx, other=0):
        return lax.rem(x + dx, SIDE) * 2 + lax.rem(core + other, 2)

    mate = sp_at(0, 1)
    group = x // 2
    ally = (x + 1 - 2 * lax.rem(x, 2)) * 2 + core
    cross = (SIDE - 1 - x) * 2 + core

    peers = [(lax.rem(z + d, SIDE) * SIDE + y, sp) for d in (1, 3)]
    peers += [(z * SIDE + lax.rem(y + d, SIDE), sp) for d in (1, 3)]
    peers += [(tp, lax.rem(sp + d, 2 * SIDE)) for d in range(1, 2 * SIDE)]
    barrier_with(peers)

    grid = Gather2D(
        (z, y), lambda u, v: (u * SIDE + v, sp),
        lambda r, h: x_ref.at[pl.ds(r * chunk, chunk), pl.ds(h * half, half)],
        lambda r, h, u, v: x_all.at[pl.ds(r * chunk, chunk), pl.ds(pl.multiple_of((u * SIDE + v) * width + h * half, half), half)],
        xs, xr)

    def w_at(owner, p):
        return w_all.at[pl.ds(pl.multiple_of(owner * depth + p * (depth // 2), depth // 2), depth // 2), :]

    w_sends = []

    def w_send(owner, p, to, src=None):
        k = len(w_sends)
        copy = remote(w_at(owner, p) if src is None else src, w_at(owner, p), ws.at[k], wr.at[owner, p], tp, to)
        copy.start()
        w_sends.append(copy)

    def w_wait(owner, p):
        arrived(w_at(owner, p), wr.at[owner, p], tp, sp)

    def w_own(p):
        src = w_ref.at[pl.ds(p * (depth // 2), depth // 2), :]
        for to in (sp_at(1), sp_at(3), mate):
            w_send(sp, p, to, src)

    def w_near(p):
        for d in (3, 1):
            w_wait(sp_at(d), p)
            if d == (3 if p == 0 else 1):
                w_send(sp_at(d), p, sp_at(4 - d))
            w_send(sp_at(d), p, mate)

    def w_far():
        for p in (0, 1):
            w_wait(sp_at(2), p)
            w_send(sp_at(2), p, mate)

    def w_mate():
        for p in (0, 1):
            for d in (0, 1, 3, 2):
                w_wait(sp_at(d, 1), p)

    grid.start(0)
    w_own(0)
    w_own(1)
    seg_copies = []
    for d in range(1, 2 * SIDE):
        copy = remote(seg_ref, segall_ref.at[sp], ss.at[d], sr.at[sp], tp, lax.rem(sp + d, 2 * SIDE))
        copy.start()
        seg_copies.append(copy)
    segall_ref[sp] = seg_ref[...]
    x_all[:, pl.ds(pl.multiple_of(tp * width, width), width)] = x_ref[...]
    w_all[pl.ds(pl.multiple_of(sp * depth, depth), depth), :] = w_ref[...]

    def kv_at(owner, r):
        return kv_ref.at[pl.ds(pl.multiple_of(owner * rows + r * chunk, chunk), chunk), :]

    kv_sends = []

    def kv_send(src, dst, recv, to):
        k = len(kv_sends)
        copy = remote(src, dst, ks.at[k], recv, tp, to)
        copy.start()
        kv_sends.append(copy)

    def project(r):
        here = slice(r * chunk, (r + 1) * chunk)
        for n in range(3):
            part = slice(n * 256, (n + 1) * 256)
            out = jnp.dot(x_all[here, :], w_all[:, part], preferred_element_type=jnp.float32).astype(jnp.bfloat16)
            for m in range(2):
                col = n * 2 + m
                qkv[col // 3, here, (col % 3) * HEAD_DIM:(col % 3 + 1) * HEAD_DIM] = out[:, m * HEAD_DIM:(m + 1) * HEAD_DIM]
        q_ref[here, :] = qkv[group, here, :HEAD_DIM]
        kv_ref[pl.ds(pl.multiple_of(sp * rows + r * chunk, chunk), chunk), :] = qkv[group, here, HEAD_DIM:]
        span = pl.ds(r * chunk, chunk)
        kv_send(qkv.at[1 - group, span, pl.ds(HEAD_DIM, 2 * HEAD_DIM)], kv_at(sp, r), kr.at[sp, r], cross)
        kv_send(qkv.at[1 - group, span, pl.ds(0, HEAD_DIM)], q_ref.at[pl.ds(rows + r * chunk, chunk), :], kr.at[2 * SIDE, r], cross)
        kv_send(qkv.at[group, span, pl.ds(HEAD_DIM, 2 * HEAD_DIM)], kv_at(sp, r), kr.at[sp, r], ally)
        kv_send(qkv.at[group, span, pl.ds(HEAD_DIM, 2 * HEAD_DIM)], kv_at(sp, r), kr.at[sp, r], mate)

    ally_cross = lax.rem(x + 2, SIDE) * 2 + core

    def kv_wait(owner, r):
        arrived(kv_at(owner, r), kr.at[owner, r], tp, sp)

    def kv_cross(r):
        kv_wait(cross, r)
        kv_send(kv_at(cross, r), kv_at(cross, r), kr.at[cross, r], ally)
        kv_send(kv_at(cross, r), kv_at(cross, r), kr.at[cross, r], mate)

    def kv_ally(r):
        for owner in (ally, ally_cross):
            kv_wait(owner, r)
            kv_send(kv_at(owner, r), kv_at(owner, r), kr.at[owner, r], mate)

    def kv_mate(r):
        arrived(q_ref.at[pl.ds(rows + r * chunk, chunk), :], kr.at[2 * SIDE, r], tp, sp)
        for d in range(SIDE):
            kv_wait(sp_at(d, 1), r)

    grid.near(0)
    grid.start(1)
    grid.far(0)
    grid.last(0)
    w_near(0)
    grid.near(1)
    grid.start(2)
    grid.far(1)
    grid.last(1)
    w_near(1)
    grid.near(2)
    grid.start(3)
    w_far()
    w_mate()
    project(0)
    grid.far(2)
    project(1)
    grid.last(2)
    kv_cross(0)
    grid.near(3)
    project(2)
    kv_cross(1)
    kv_ally(0)
    grid.far(3)
    kv_ally(1)
    kv_cross(2)
    grid.last(3)
    project(3)
    kv_ally(2)
    kv_cross(3)
    kv_ally(3)
    for r in range(CHUNKS):
        kv_mate(r)
    for d in range(1, 2 * SIDE):
        arrived(segall_ref.at[lax.rem(sp + d, 2 * SIDE)], sr.at[lax.rem(sp + d, 2 * SIDE)], tp, sp)
    for r in range(CHUNKS):
        grid.drain(r)
    for copy in w_sends + seg_copies + kv_sends:
        copy.wait_send()


def qkv_exchange(x_block, wqkv_block, seg_block):
    rows, width = x_block.shape
    depth, cols = wqkv_block.shape
    sps, tps = 2 * SIDE, SIDE * SIDE
    seg_tile = seg_block.reshape(rows // HEAD_DIM, HEAD_DIM)
    vmem = pl.BlockSpec(memory_space=pltpu.VMEM)
    dma = pltpu.SemaphoreType.DMA
    return pl.pallas_call(
        qkv_kernel,
        out_shape=(
            jax.ShapeDtypeStruct((2 * rows, HEAD_DIM), jnp.bfloat16),
            jax.ShapeDtypeStruct((sps * rows, 2 * HEAD_DIM), jnp.bfloat16),
            jax.ShapeDtypeStruct((sps,) + seg_tile.shape, jnp.int32),
        ),
        in_specs=[vmem] * 3,
        out_specs=(vmem,) * 3,
        scratch_shapes=[
            pltpu.VMEM((rows, tps * width), jnp.bfloat16),
            pltpu.VMEM((sps * depth, cols), jnp.bfloat16),
            pltpu.VMEM((2, rows, 3 * HEAD_DIM), jnp.bfloat16),
            dma((CHUNKS, 2, 15)), dma((CHUNKS, 2, tps)),
            dma((14,)), dma((sps, 2)),
            dma((sps,)), dma((sps,)),
            dma((8 * CHUNKS,)), dma((sps + 1, CHUNKS)),
        ],
        compiler_params=pltpu.CompilerParams(collective_id=0, has_side_effects=True, vmem_limit_bytes=56 * 1024 * 1024),
        name="qkv_exchange",
    )(x_block, wqkv_block, seg_tile)


def output_kernel(ctx_ref, w_ref, y_ref, o_all, w_all, part, os, orr, ws, wr, ms, mr, ys, yr):
    tp, sp = lax.axis_index("tp"), lax.axis_index("sp")
    z, y = tp // SIDE, lax.rem(tp, SIDE)
    x, core = sp // 2, lax.rem(sp, 2)
    rows = ctx_ref.shape[0] // 2
    quarter = rows // SIDE
    depth, width = w_ref.shape
    group = x // 2
    cross = (SIDE - 1 - x) * 2 + core
    mate = x * 2 + 1 - core

    def x_at(d):
        return lax.rem(x + d, SIDE) * 2 + core

    def z_at(d):
        return lax.rem(z + d, SIDE)

    def y_at(d):
        return lax.rem(y + d, SIDE)

    peers = [(z_at(d) * SIDE + y, sp) for d in (1, 2, 3)]
    peers += [(z_at(d) * SIDE + y, cross) for d in range(SIDE)]
    peers += [(z * SIDE + y_at(d), sp) for d in (1, 2, 3)]
    peers += [(tp, x_at(1)), (tp, x_at(3)), (tp, mate)]
    barrier_with(peers)

    o_sends = []

    def o_slot(j, yo, b):
        return (z_at(j) * SIDE + yo) * 2 + (group if b == 0 else 1 - group)

    def o_col(slot):
        return o_all.at[:, pl.ds(pl.multiple_of(slot * HEAD_DIM, HEAD_DIM), HEAD_DIM)]

    def o_send(src, slot, to_tp, to_sp):
        copy = remote(src, o_col(slot), os.at[len(o_sends)], orr.at[slot], to_tp, to_sp)
        copy.start()
        o_sends.append(copy)

    def o_wait(slot):
        arrived(o_col(slot), orr.at[slot], tp, sp)

    def ctx_rows(j, b):
        return ctx_ref.at[pl.ds(pl.multiple_of(b * rows + z_at(j) * quarter, quarter), quarter), :]

    def o_along_y(j, b, src):
        slot = o_slot(j, y, b)
        for d in (1, 3):
            o_send(src, slot, z * SIDE + y_at(d), sp)

    mine = (z * SIDE + y) * 2 + group
    order = [(0, 1), (1, 0), (3, 0), (1, 1), (3, 1), (2, 0), (2, 1)]
    for j, b in order:
        o_send(ctx_rows(j, b), mine, z_at(j) * SIDE + y, sp if b == 0 else cross)
    o_along_y(0, 0, ctx_rows(0, 0))
    o_all[:, pl.ds(pl.multiple_of(mine * HEAD_DIM, HEAD_DIM), HEAD_DIM)] = ctx_ref[pl.ds(pl.multiple_of(z * quarter, quarter), quarter), :]

    steps = 2
    chunk = depth // steps
    half = width // 2
    grid = Gather2D(
        (x, z), lambda u, v: (v * SIDE + y, u * 2 + core),
        lambda r, h: w_ref.at[pl.ds(r * chunk, chunk), pl.ds(h * half, half)],
        lambda r, h, u, v: w_all.at[pl.ds(pl.multiple_of((u * 2 + core) * depth + r * chunk, chunk), chunk),
                                    pl.ds(pl.multiple_of(v * width + h * half, half), half)],
        ws, wr)
    w_all[pl.ds(pl.multiple_of(sp * depth, depth), depth), pl.ds(pl.multiple_of(z * width, width), width)] = w_ref[...]

    def o_near(j, b):
        for d in (3, 1):
            slot = o_slot(j, y_at(d), b)
            o_wait(slot)
            if d == (3 if (j + b) % 2 == 0 else 1):
                o_send(o_col(slot), slot, z * SIDE + y_at(4 - d), sp)

    def o_first(j, b):
        o_wait(o_slot(j, y, b))
        o_along_y(j, b, o_col(o_slot(j, y, b)))

    m_sends = []

    def m_at(sx, other, dz, r):
        owner = lax.rem(x + sx, SIDE) * 2 + (1 - core if other else core)
        return w_all.at[pl.ds(pl.multiple_of(owner * depth + r * chunk, chunk), chunk),
                        pl.ds(pl.multiple_of(z_at(dz) * width, width), width)]

    def m_slot(sx, dz):
        return lax.rem(x + sx, SIDE) * SIDE + z_at(dz)

    def w_mate(r):
        for sx in range(SIDE):
            for dz in range(SIDE):
                src = w_ref.at[pl.ds(r * chunk, chunk), :] if (sx, dz) == (0, 0) else m_at(sx, False, dz, r)
                copy = remote(src, m_at(sx, False, dz, r), ms.at[len(m_sends)], mr.at[m_slot(sx, dz), r], tp, mate)
                copy.start()
                m_sends.append(copy)

    grid.start(0)
    for j, b in order[:3]:
        o_first(j, b)
    o_near(0, 0)
    grid.near(0)
    grid.start(1)
    for j, b in order[3:]:
        o_first(j, b)
    for j, b in order[:2]:
        o_near(j, b)
    grid.far(0)
    for j, b in order[2:4]:
        o_near(j, b)
    grid.last(0)
    w_mate(0)
    for j, b in order[4:]:
        o_near(j, b)
    grid.near(1)
    grid.far(1)
    grid.last(1)
    w_mate(1)
    for j, b in [(0, 0)] + order:
        o_wait(o_slot(j, y_at(2), b))
    for r in range(steps):
        for sx in range(SIDE):
            for dz in range(SIDE):
                arrived(m_at(sx, True, dz, r), mr.at[m_slot(sx, dz), r], tp, sp)

    y_sends = []
    strip = quarter // SIDE
    for zz in range(SIDE):
        out = jnp.dot(o_all[...], w_all[:, zz * width:(zz + 1) * width], preferred_element_type=jnp.float32)
        part[zz] = out.astype(jnp.bfloat16)
        cols = pl.ds(pl.multiple_of((zz * SIDE + y) * width, width), width)
        for d in (2, 1, 3):
            copy = remote(part.at[zz, pl.ds(pl.multiple_of(y_at(d) * strip, strip), strip), :], y_ref.at[:, cols],
                          ys.at[len(y_sends)], yr.at[zz, y], z * SIDE + y_at(d), sp)
            copy.start()
            y_sends.append(copy)
        y_ref[:, cols] = part[zz, pl.ds(pl.multiple_of(y * strip, strip), strip), :]
    for zz in range(SIDE):
        for d in (1, 3, 2):
            cols = pl.ds(pl.multiple_of((zz * SIDE + y_at(d)) * width, width), width)
            arrived(y_ref.at[:, cols], yr.at[zz, y_at(d)], tp, sp)
    for r in range(steps):
        grid.drain(r)
    for copy in o_sends + m_sends + y_sends:
        copy.wait_send()


def output_exchange(context, wout_block):
    rows = context.shape[0] // 2
    depth, width = wout_block.shape
    sps, tps = 2 * SIDE, SIDE * SIDE
    quarter = rows // SIDE
    vmem = pl.BlockSpec(memory_space=pltpu.VMEM)
    dma = pltpu.SemaphoreType.DMA
    return pl.pallas_call(
        output_kernel,
        out_shape=jax.ShapeDtypeStruct((quarter // SIDE, tps * width), jnp.bfloat16),
        in_specs=[vmem] * 2,
        out_specs=vmem,
        scratch_shapes=[
            pltpu.VMEM((quarter, tps * 2 * HEAD_DIM), jnp.bfloat16),
            pltpu.VMEM((sps * depth, SIDE * width), jnp.bfloat16),
            pltpu.VMEM((SIDE, quarter, width), jnp.bfloat16),
            dma((31,)), dma((2 * tps,)),
            dma((2, 2, 15)), dma((2, 2, tps)),
            dma((2 * tps,)), dma((tps, 2)),
            dma((3 * SIDE,)), dma((SIDE, SIDE)),
        ],
        compiler_params=pltpu.CompilerParams(collective_id=1, has_side_effects=True, vmem_limit_bytes=56 * 1024 * 1024),
        name="output_exchange",
    )(context, wout_block)


def solution(mesh):
    def device_block(x_block, doc_block, wqkv_block, wout_block):
        rows = x_block.shape[0]
        q, kv, seg_all = qkv_exchange(x_block, wqkv_block, doc_block)
        seg_all = seg_all.reshape(-1)
        sp = lax.axis_index("sp")
        cross = (SIDE - 1 - sp // 2) * 2 + sp % 2
        seg_q = jnp.concatenate([doc_block, lax.dynamic_slice(seg_all, (cross * rows,), (rows,))])
        context = attention(q, kv, seg_q, seg_all)
        return output_exchange(context, wout_block)

    return jax.shard_map(
        device_block,
        mesh=mesh,
        in_specs=(P(("dp", "sp"), "tp"), P(("dp", "sp")), P("sp", "tp"), P("sp", "tp")),
        out_specs=P(("dp", "sp", "tp"), None),
        check_vma=False,
    )
```

profile of v0, /device:TPU:1, one launch (start us, length us, event | category | flops | bytes accessed | tf_op | source)
XLA Modules:
  0.0 191.6 jit_solution(16425641431839326163)
XLA Ops:
  0.0 94.4 %qkv_exchange.1 = (bf16[2048,128]{1,0:T(8,128)(2,1)}, bf16[8192,256]{1,0:T(8,128)(2,1)}, s32[8,8,128]{2,1,0:T(8,128)}) custom-call(bf16[1024,256]{1,0:T(8,128)(2,1)} %x_ref.1, bf16[512,768]{1,0:T(8,128)(2,1)} %w_ref.2, s32[8,128]{1,0:T(8,128)} %bitcast.9), custom_call_target="tpu_custom_call" | custom-call | tf_op jit(solution)/shard_map/qkv_exchange/pallas_call | solution.py:355
  94.4 0.7 dynamic_slice.3
  95.1 0.7 pad_add_fusion.segq_ref
  95.7 0.0 copy-start
  95.7 2.2 %copy-done = bf16[8192,256]{1,0:T(8,128)(2,1)S(1)} copy-done((bf16[8192,256]{1,0:T(8,128)(2,1)S(1)}, bf16[8192,256]{1,0:T(8,128)(2,1)}, u32[]{:S(2)}) %copy-start) | copy-done | bytes 4194328
  97.9 0.0 copy-start.2
  97.9 1.0 copy-done.2
  99.0 0.0 copy-start.3
  99.0 0.8 copy-done.3
  99.7 31.5 %attention.1.ctx_ref = bf16[2048,128]{1,0:T(8,128)(2,1)S(1)} custom-call(bf16[2048,128]{1,0:T(8,128)(2,1)S(1)} %copy-done.2, bf16[8192,256]{1,0:T(8,128)(2,1)S(1)} %copy-done, s32[4,1,512]{2,1,0:T(1,128)S(1)} %pad_add_fusion.segq_ref, s32[16,1,512]{2,1,0:T(1,128)S(1)} %bitcast.7, s32[64,128]{1,0:T(8,128)S(1)} %bitcast.8), custom_call_target="tpu_custom_call" | custom-call | tf_op jit(solution)/shard_map/attention/pallas_call | solution.py:71
  131.2 0.0 copy-start.1
  131.2 0.8 copy-done.1
  132.0 57.7 %output_exchange.1 = bf16[64,4096]{1,0:T(8,128)(2,1)} custom-call(bf16[2048,128]{1,0:T(8,128)(2,1)} %copy-done.1, bf16[512,256]{1,0:T(8,128)(2,1)} %w_ref.3), custom_call_target="tpu_custom_call" | custom-call | tf_op jit(solution)/shard_map/output_exchange/pallas_call | solution.py:532
  189.7 1.9 copy.6
Async XLA Ops:
  95.7 2.2 %copy-start = (bf16[8192,256]{1,0:T(8,128)(2,1)S(1)}, bf16[8192,256]{1,0:T(8,128)(2,1)}, u32[]{:S(2)}) copy-start(bf16[8192,256]{1,0:T(8,128)(2,1)} %get-tuple-element.9.kv_ref) | copy-start | bytes 12582916
  97.9 1.0 copy-start.2
  99.0 0.8 copy-start.3
  131.2 0.8 copy-start.1
where the time goes:
time: 193 us; the launch traced here: 192 us
  Pallas kernels  184 us (95%)
  local copies, waits for them, and re-layouts  7.33 us (4%)
    pallas_call x1, Pallas kernels, qkv_exchange(): pl.pallas_call(qkv_kernel, out_shape=(jax.ShapeDtypeStruct((2 * rows, HEA...  94.4 us
    pallas_call x1, Pallas kernels, output_exchange(): pl.pallas_call(output_kernel, out_shape=jax.ShapeDtypeStruct((quarter //...  57.7 us
    pallas_call x1, Pallas kernels, attention(): pl.pallas_call(functools.partial(attention_kernel, qb, kb, sub), grid=(he...  31.5 us
    unnamed x9, local copies, waits for them, and re-layouts  6.64 us

commit v1 on v0

--- a/solution.py
+++ b/solution.py
@@ -10,46 +10,87 @@
 HEAD_DIM = 128
 EXP2_SCALE = HEAD_DIM ** -0.5 * 1.4426950408889634
 FLOOR = -3.0e38
-
-
-def attention_kernel(qb, kb, sub, q_ref, kv_ref, segq_ref, segk_ref, segall_ref, o_ref, acc_ref, m_ref, l_ref):
-    segq_row = segq_ref[0]
-    lo = jnp.min(segq_row)
-    hi = jnp.max(segq_row)
+SMALL = 2.0 ** -77
+
+
+def seg_column(segq_ref, base, rows):
+    tiles = [jnp.broadcast_to(segq_ref[pl.ds(base + i, 1), :], (HEAD_DIM, HEAD_DIM)).T for i in range(rows // HEAD_DIM)]
+    return jnp.concatenate(tiles, axis=0)
+
+
+def attention_kernel(qb, kb, sub, q_ref, kv_ref, segq_ref, segall_ref, o_ref, q2_ref, acc_ref, m_ref, l_ref, kmax_ref, segc_ref):
+    step_id = pl.program_id(0)
+    keys = kv_ref.shape[0]
+    qrow = step_id * (qb // HEAD_DIM)
+
+    @pl.when(step_id == 0)
+    def _():
+        def norms(j, best):
+            k = kv_ref[pl.ds(pl.multiple_of(j * 2048, 2048), 2048), :HEAD_DIM].astype(jnp.float32)
+            total = jnp.dot((k * k).astype(jnp.bfloat16), jnp.ones((HEAD_DIM, HEAD_DIM), jnp.bfloat16), preferred_element_type=jnp.float32)
+            return jnp.maximum(best, jnp.max(total, axis=0, keepdims=True))
+
+        kmax_ref[...] = jnp.broadcast_to(jnp.sqrt(lax.fori_loop(0, keys // 2048, norms, jnp.zeros((1, HEAD_DIM), jnp.float32))), kmax_ref.shape)
+
+    segq = segq_ref[pl.ds(qrow, qb // HEAD_DIM), :]
+    lo = jnp.min(segq)
+    hi = jnp.max(segq)
     seg_all = segall_ref[...]
     first = jnp.sum(jnp.where(seg_all < lo, 1.0, 0.0)).astype(jnp.int32)
     last = jnp.sum(jnp.where(seg_all <= hi, 1.0, 0.0)).astype(jnp.int32)
     one_doc = lo == hi
-
+    whole_rows = first // HEAD_DIM * HEAD_DIM
+    count = (last - whole_rows + kb - 1) // kb
+    base = jnp.minimum(whole_rows, keys - count * kb)
+
+    q = q_ref[...]
+    qf = q.astype(jnp.float32)
+    bound = jnp.sqrt(jnp.sum(qf * qf, axis=1, keepdims=True)) * kmax_ref[:1, :] * (-1.01 / HEAD_DIM)
+    q2_ref[:, :HEAD_DIM] = q
+    q2_ref[:, HEAD_DIM:] = bound.astype(jnp.bfloat16)
     acc_ref[...] = jnp.zeros_like(acc_ref)
-    l_ref[...] = jnp.zeros_like(l_ref)
-    m_ref[...] = jnp.full_like(m_ref, FLOOR)
+    segc_ref[...] = seg_column(segq_ref, qrow, qb)
+
+    def same_doc(j, rows):
+        row = jnp.concatenate([segall_ref[pl.ds(base // HEAD_DIM + j * (kb // HEAD_DIM) + i, 1), :] for i in range(kb // HEAD_DIM)], axis=1)
+        return segc_ref[rows, :1] == row
+
+    def pieces(j):
+        start = pl.multiple_of(base + j * kb, HEAD_DIM)
+        return kv_ref[pl.ds(start, kb), :HEAD_DIM], kv_ref[pl.ds(start, kb), HEAD_DIM:]
+
+    ones = jnp.ones((kb, HEAD_DIM), jnp.bfloat16)
 
     def block(j, masked):
-        start = pl.multiple_of(j * kb, kb)
-        k = kv_ref[pl.ds(start, kb), :HEAD_DIM]
-        v = kv_ref[pl.ds(start, kb), HEAD_DIM:]
-        if masked:
-            segk_row = segk_ref[j]
+        k, v = pieces(j)
+        k2 = jnp.concatenate([k, ones], axis=1)
+        v2 = jnp.concatenate([v, ones], axis=1)
+        for i in range(qb // sub):
+            rows = slice(i * sub, (i + 1) * sub)
+            s = lax.dot_general(q2_ref[rows, :], k2, (((1,), (1,)), ((), ())), preferred_element_type=jnp.float32)
+            p = jnp.exp2(s * EXP2_SCALE)
+            if masked:
+                p = jnp.where(same_doc(j, rows), p, 0.0)
+            acc_ref[rows, :] += jnp.dot(p.astype(jnp.bfloat16), v2, preferred_element_type=jnp.float32)
+
+    def online(j, masked):
+        k, v = pieces(j)
         for i in range(qb // sub):
             rows = slice(i * sub, (i + 1) * sub)
             s = lax.dot_general(q_ref[rows, :], k, (((1,), (1,)), ((), ())), preferred_element_type=jnp.float32)
-            t = s * EXP2_SCALE
-            if masked:
-                segq_col = jnp.broadcast_to(segq_row[:, rows], (HEAD_DIM, sub)).T
-                t = jnp.where(segq_col[:, :1] == segk_row, t, -jnp.inf)
+            t = jnp.where(same_doc(j, rows), s * EXP2_SCALE, -jnp.inf)
             m_prev = m_ref[rows, :1]
             m_new = jnp.maximum(m_prev, jnp.max(t, axis=1, keepdims=True))
             p = jnp.exp2(t - m_new)
             alpha = jnp.exp2(m_prev - m_new)
             l_new = l_ref[rows, :1] * alpha + jnp.sum(p, axis=1, keepdims=True)
             pv = jnp.dot(p.astype(jnp.bfloat16), v, preferred_element_type=jnp.float32)
-            acc_ref[rows, :] = acc_ref[rows, :] * alpha + pv
+            acc_ref[rows, :HEAD_DIM] = acc_ref[rows, :HEAD_DIM] * alpha + pv
             m_ref[rows, :] = jnp.broadcast_to(m_new, (sub, HEAD_DIM))
             l_ref[rows, :] = jnp.broadcast_to(l_new, (sub, HEAD_DIM))
 
     def step(j, carry):
-        whole = one_doc & (j * kb >= first) & ((j + 1) * kb <= last)
+        whole = one_doc & (base + j * kb >= first) & (base + (j + 1) * kb <= last)
 
         @pl.when(whole)
         def _():
@@ -61,34 +102,45 @@
 
         return carry
 
-    lax.fori_loop(first // kb, (last + kb - 1) // kb, step, 0)
-    o_ref[...] = (acc_ref[...] / l_ref[...]).astype(o_ref.dtype)
-
-
-def attention(q, kv, seg_q, seg_all, qb=512, kb=512, sub=256):
+    lax.fori_loop(0, count, step, 0)
+    total = acc_ref[:, HEAD_DIM:]
+    o_ref[...] = (acc_ref[:, :HEAD_DIM] / total).astype(o_ref.dtype)
+
+    @pl.when(jnp.logical_not(jnp.min(total) >= SMALL))
+    def _():
+        acc_ref[...] = jnp.zeros_like(acc_ref)
+        l_ref[...] = jnp.zeros_like(l_ref)
+        m_ref[...] = jnp.full_like(m_ref, FLOOR)
+
+        def again(j, carry):
+            online(j, True)
+            return carry
+
+        lax.fori_loop(0, count, again, 0)
+        o_ref[...] = (acc_ref[:, :HEAD_DIM] / l_ref[...]).astype(o_ref.dtype)
+
+
+def attention(q, kv, seg_q, seg_all, qb=1024, kb=1024, sub=256):
     rows, keys = q.shape[0], kv.shape[0]
-    heads = q.shape[1] // HEAD_DIM
+    whole = lambda a: pl.BlockSpec(a, lambda i: (0, 0))
+    f32 = lambda *shape: pltpu.VMEM(shape, jnp.float32)
     return pl.pallas_call(
         functools.partial(attention_kernel, qb, kb, sub),
-        grid=(heads, rows // qb),
+        grid=(rows // qb,),
         out_shape=jax.ShapeDtypeStruct(q.shape, jnp.bfloat16),
         in_specs=[
-            pl.BlockSpec((qb, HEAD_DIM), lambda h, i: (i, h)),
-            pl.BlockSpec((keys, 2 * HEAD_DIM), lambda h, i: (0, h)),
-            pl.BlockSpec((1, 1, qb), lambda h, i: (i, 0, 0)),
-            pl.BlockSpec((keys // kb, 1, kb), lambda h, i: (0, 0, 0)),
-            pl.BlockSpec((keys // HEAD_DIM, HEAD_DIM), lambda h, i: (0, 0)),
+            pl.BlockSpec((qb, HEAD_DIM), lambda i: (i, 0)),
+            whole(kv.shape), whole(seg_q.shape), whole(seg_all.shape),
         ],
-        out_specs=pl.BlockSpec((qb, HEAD_DIM), lambda h, i: (i, h)),
+        out_specs=pl.BlockSpec((qb, HEAD_DIM), lambda i: (i, 0)),
         scratch_shapes=[
-            pltpu.VMEM((qb, HEAD_DIM), jnp.float32),
-            pltpu.VMEM((qb, HEAD_DIM), jnp.float32),
-            pltpu.VMEM((qb, HEAD_DIM), jnp.float32),
+            pltpu.VMEM((qb, 2 * HEAD_DIM), jnp.bfloat16),
+            f32(qb, 2 * HEAD_DIM), f32(qb, HEAD_DIM), f32(qb, HEAD_DIM), f32(8, HEAD_DIM),
+            pltpu.VMEM((qb, HEAD_DIM), jnp.int32),
         ],
-        compiler_params=pltpu.CompilerParams(vmem_limit_bytes=48 * 1024 * 1024),
+        compiler_params=pltpu.CompilerParams(vmem_limit_bytes=24 * 1024 * 1024),
         name="attention",
-    )(q, kv, seg_q.reshape(rows // qb, 1, qb), seg_all.reshape(keys // kb, 1, kb), seg_all.reshape(keys // HEAD_DIM, HEAD_DIM))
-
+    )(q, kv, seg_q, seg_all)
 
 SIDE = 4
 CHUNKS = 4
@@ -169,6 +221,8 @@
     def last(self, r):
         for j1 in (3, 1, 2):
             self.pass_on(r, j1)
+
+    def final(self, r):
         for j1 in (0, 3, 1, 2):
             for h in (0, 1):
                 self.wait(r, h, (j1, 2))
@@ -180,7 +234,7 @@
                 remote(ref, ref, self.send_sem.at[r, h, k], self.recv_sem.at[r, h, 0], *self.place(*self.coords)).wait_send()
 
 
-def qkv_kernel(x_ref, w_ref, seg_ref, q_ref, kv_ref, segall_ref,
+def qkv_kernel(x_ref, w_ref, seg_ref, q_ref, kv_ref, segall_ref, segq_ref,
                x_all, w_all, qkv, xs, xr, ws, wr, ss, sr, ks, kr):
     tp, sp = lax.axis_index("tp"), lax.axis_index("sp")
     z, y = tp // SIDE, lax.rem(tp, SIDE)
@@ -247,7 +301,6 @@
 
     grid.start(0)
     w_own(0)
-    w_own(1)
     seg_copies = []
     for d in range(1, 2 * SIDE):
         copy = remote(seg_ref, segall_ref.at[sp], ss.at[d], sr.at[sp], tp, lax.rem(sp + d, 2 * SIDE))
@@ -305,32 +358,37 @@
             kv_wait(sp_at(d, 1), r)
 
     grid.near(0)
+    w_own(1)
     grid.start(1)
     grid.far(0)
+    grid.near(1)
     grid.last(0)
     w_near(0)
-    grid.near(1)
     grid.start(2)
     grid.far(1)
+    grid.near(2)
+    w_near(1)
     grid.last(1)
-    w_near(1)
-    grid.near(2)
     grid.start(3)
+    grid.far(2)
     w_far()
     w_mate()
+    grid.final(0)
     project(0)
-    grid.far(2)
+    grid.near(3)
+    grid.final(1)
     project(1)
     grid.last(2)
     kv_cross(0)
-    grid.near(3)
-    project(2)
+    grid.far(3)
     kv_cross(1)
     kv_ally(0)
-    grid.far(3)
+    grid.final(2)
+    project(2)
     kv_ally(1)
+    grid.last(3)
     kv_cross(2)
-    grid.last(3)
+    grid.final(3)
     project(3)
     kv_ally(2)
     kv_cross(3)
@@ -339,6 +397,8 @@
         kv_mate(r)
     for d in range(1, 2 * SIDE):
         arrived(segall_ref.at[lax.rem(sp + d, 2 * SIDE)], sr.at[lax.rem(sp + d, 2 * SIDE)], tp, sp)
+    segq_ref[0] = seg_ref[...]
+    segq_ref[1] = segall_ref[cross]
     for r in range(CHUNKS):
         grid.drain(r)
     for copy in w_sends + seg_copies + kv_sends:
@@ -358,9 +418,10 @@
             jax.ShapeDtypeStruct((2 * rows, HEAD_DIM), jnp.bfloat16),
             jax.ShapeDtypeStruct((sps * rows, 2 * HEAD_DIM), jnp.bfloat16),
             jax.ShapeDtypeStruct((sps,) + seg_tile.shape, jnp.int32),
+            jax.ShapeDtypeStruct((2,) + seg_tile.shape, jnp.int32),
         ),
         in_specs=[vmem] * 3,
-        out_specs=(vmem,) * 3,
+        out_specs=(vmem,) * 4,
         scratch_shapes=[
             pltpu.VMEM((rows, tps * width), jnp.bfloat16),
             pltpu.VMEM((sps * depth, cols), jnp.bfloat16),
@@ -370,7 +431,7 @@
             dma((sps,)), dma((sps,)),
             dma((8 * CHUNKS,)), dma((sps + 1, CHUNKS)),
         ],
-        compiler_params=pltpu.CompilerParams(collective_id=0, has_side_effects=True, vmem_limit_bytes=56 * 1024 * 1024),
+        compiler_params=pltpu.CompilerParams(collective_id=0, has_side_effects=True, vmem_limit_bytes=26 * 1024 * 1024),
         name="qkv_exchange",
     )(x_block, wqkv_block, seg_tile)
 
@@ -486,12 +547,14 @@
     for j, b in order[2:4]:
         o_near(j, b)
     grid.last(0)
+    grid.final(0)
     w_mate(0)
     for j, b in order[4:]:
         o_near(j, b)
     grid.near(1)
     grid.far(1)
     grid.last(1)
+    grid.final(1)
     w_mate(1)
     for j, b in [(0, 0)] + order:
         o_wait(o_slot(j, y_at(2), b))
@@ -543,20 +606,15 @@
             dma((2 * tps,)), dma((tps, 2)),
             dma((3 * SIDE,)), dma((SIDE, SIDE)),
         ],
-        compiler_params=pltpu.CompilerParams(collective_id=1, has_side_effects=True, vmem_limit_bytes=56 * 1024 * 1024),
+        compiler_params=pltpu.CompilerParams(collective_id=1, has_side_effects=True, vmem_limit_bytes=16 * 1024 * 1024),
         name="output_exchange",
     )(context, wout_block)
 
 
 def solution(mesh):
     def device_block(x_block, doc_block, wqkv_block, wout_block):
-        rows = x_block.shape[0]
-        q, kv, seg_all = qkv_exchange(x_block, wqkv_block, doc_block)
-        seg_all = seg_all.reshape(-1)
-        sp = lax.axis_index("sp")
-        cross = (SIDE - 1 - sp // 2) * 2 + sp % 2
-        seg_q = jnp.concatenate([doc_block, lax.dynamic_slice(seg_all, (cross * rows,), (rows,))])
-        context = attention(q, kv, seg_q, seg_all)
+        q, kv, seg_all, seg_q = qkv_exchange(x_block, wqkv_block, doc_block)
+        context = attention(q, kv, seg_q.reshape(-1, HEAD_DIM), seg_all.reshape(-1, HEAD_DIM))
         return output_exchange(context, wout_block)
 
     return jax.shard_map(

time: 193 us -> 169 us (0.88)
  Pallas kernels: 184 us -> 165 us
  local copies, waits for them, and re-layouts: 7.33 us -> 3.66 us
    pallas_call x1, Pallas kernels: 31.5 us -> 10.2 us  [attention(): pl.pallas_call(functools.partial(attention_kernel, qb, kb, sub), grid=(ro...]
    pallas_call x1, Pallas kernels: 57.7 us -> 78.1 us  [output_exchange(): pl.pallas_call(output_kernel, out_shape=jax.ShapeDtypeStruct((quarter //...]
    pallas_call x1, Pallas kernels: 94.4 us -> 77 us  [qkv_exchange(): pl.pallas_call(qkv_kernel, out_shape=(jax.ShapeDtypeStruct((2 * rows, HEA...]
    unnamed x9, local copies, waits for them, and re-layouts: 6.64 us -> 3.66 us
where the time goes in v1:
time: 169 us
  Pallas kernels  165 us (98%)
  local copies, waits for them, and re-layouts  3.66 us (2%)
    pallas_call x1, Pallas kernels, output_exchange(): pl.pallas_call(output_kernel, out_shape=jax.ShapeDtypeStruct((quarter //...  78.1 us
    pallas_call x1, Pallas kernels, qkv_exchange(): pl.pallas_call(qkv_kernel, out_shape=(jax.ShapeDtypeStruct((2 * rows, HEA...  77 us
    pallas_call x1, Pallas kernels, attention(): pl.pallas_call(functools.partial(attention_kernel, qb, kb, sub), grid=(ro...  10.2 us
    unnamed x9, local copies, waits for them, and re-layouts  3.66 us

profile of v1, /device:TPU:1, one launch (start us, length us, event | category | flops | bytes accessed | tf_op | source)
XLA Modules:
  0.0 169.1 jit_solution(10219339063721744041)
XLA Ops:
  0.0 0.0 copy-start
  0.0 1.1 copy-done
  1.1 0.0 copy-start.1
  1.1 1.0 copy-done.1
  2.2 0.0 copy-start.3
  2.2 0.7 copy-done.3
  2.9 0.0 copy-start.2
  2.9 77.0 %qkv_exchange.1 = (bf16[2048,128]{1,0:T(8,128)(2,1)S(1)}, bf16[8192,256]{1,0:T(8,128)(2,1)S(1)}, s32[8,8,128]{2,1,0:T(8,128)S(1)}, s32[2,8,128]{2,1,0:T(8,128)S(1)}) custom-call(bf16[1024,256]{1,0:T(8,128)(2,1)S(1)} %copy-done.1, bf16[512,768]{1,0:T(8,128)(2,1)S(1)} %copy-done, s32[8,128]{1,0:T(8,128)S(1)} %bitcast.5), custom_call_target="tpu_custom_call" | custom-call | tf_op jit(solution)/shard_map/qkv_exchange/pallas_call | solution.py:415
  79.9 10.2 %attention.1.ctx_ref = bf16[2048,128]{1,0:T(8,128)(2,1)S(1)} custom-call(bf16[2048,128]{1,0:T(8,128)(2,1)S(1)} %get-tuple-element.9.q_ref, bf16[8192,256]{1,0:T(8,128)(2,1)S(1)} %get-tuple-element.10.kv_ref, s32[16,128]{1,0:T(8,128)S(1)} %bitcast.4, s32[64,128]{1,0:T(8,128)S(1)} %bitcast.3), custom_call_target="tpu_custom_call" | custom-call | tf_op jit(solution)/shard_map/attention/pallas_call | solution.py:127
  90.1 0.0 copy-done.2
  90.1 78.1 %output_exchange.1 = bf16[64,4096]{1,0:T(8,128)(2,1)S(1)} custom-call(bf16[2048,128]{1,0:T(8,128)(2,1)S(1)} %attention.1.ctx_ref, bf16[512,256]{1,0:T(8,128)(2,1)S(1)} %copy-done.2), custom_call_target="tpu_custom_call" | custom-call | tf_op jit(solution)/shard_map/output_exchange/pallas_call | solution.py:595
  168.3 0.8 copy.6
Async XLA Ops:
  0.0 1.1 copy-start
  1.1 1.0 copy-start.1
  2.2 0.7 copy-start.3
  2.9 87.3 %copy-start.2 = (bf16[512,256]{1,0:T(8,128)(2,1)S(1)}, bf16[512,256]{1,0:T(8,128)(2,1)}, u32[]{:S(2)}) copy-start(bf16[512,256]{1,0:T(8,128)(2,1)} %w_ref.3) | copy-start | bytes 786436
